TPU v7x, 32 devices: a whole 2x2x4 slice. The times are simulated.
32 devices in a mesh: dp: 8 (over y, x, core), mp: 4 (over z).
Axes of the slice: x: 2, y: 2, z: 4, core: 2. Of those that a mesh axis runs over, the one named last changes fastest.
Arguments:
- layer_input: bfloat16 [32, 8192], P('dp'), may hold values from -6 to 6
- pre_act: bfloat16 [32, 8192], P('dp', 'mp'), may hold values from -8 to 8
- hidden_adjoint: bfloat16 [32, 8192], P('dp', 'mp'), may hold values from -6 to 6
- output_adjoint: bfloat16 [32, 8192], P('dp', 'mp'), may hold values from -6 to 6
Outputs:
- precond_in: float32 [8192, 8192], P('dp', 'mp')
- direction_in: float32 [8192, 8192], P('dp', 'mp')
- precond_out: float32 [8192, 8192], P('dp', 'mp')
- direction_out: float32 [8192, 8192], P('dp', 'mp')
- sq_norm: float32 [], replicated
All inputs are finite; a program needn't handle non-finite values.
Results may differ from a plain program's by a relative error of at most 0.0029.
Values may be sent and summed in bfloat16 or wider, within the bound.
A program may use at most 64 MiB of HBM per device.

v0:
```python
import jax
import jax.numpy as jnp
from jax import lax
from jax.sharding import PartitionSpec as P

D = 8192
H = 8192


DAMPING = 0.1
EXPONENT = 0.75


def square_bf(values):
    wide = values.astype(jnp.float32)
    return (wide * wide).astype(jnp.bfloat16)


def accumulate(act_block, sq_block, adj_piece):
    contract = (((0,), (0,)), ((), ()))
    grad_sum = lax.dot_general(act_block, adj_piece, contract, preferred_element_type=jnp.float32)
    square_sum = lax.dot_general(
        sq_block, square_bf(adj_piece), contract, preferred_element_type=jnp.float32
    )
    return (grad_sum, square_sum)


def finish(partial_value, total_rows):
    gradient = partial_value[0] / total_rows
    precond = (partial_value[1] / total_rows + DAMPING) ** EXPONENT
    norm_term = jnp.sum(gradient * gradient / precond)
    return (gradient, precond, norm_term)


def shards(layer_input, pre_act, hidden_adjoint, output_adjoint):
    preact = pre_act.astype(jnp.float32)
    logistic = jax.nn.sigmoid(preact)
    hidden = (preact * logistic).astype(jnp.bfloat16)
    adjoint = (
        hidden_adjoint.astype(jnp.float32) * logistic * (1.0 + preact * (1.0 - logistic))
    ).astype(jnp.bfloat16)
    own_input = lax.all_to_all(layer_input, "dp", split_axis=1, concat_axis=0, tiled=True)
    sq_input = square_bf(own_input)
    total_rows = own_input.shape[0]
    wide_hidden = lax.all_gather(hidden, "mp", axis=1, tiled=True)
    own_hidden = lax.all_to_all(wide_hidden, "dp", split_axis=1, concat_axis=0, tiled=True)
    sq_hidden = square_bf(own_hidden)
    sums_in = accumulate(own_input, sq_input, lax.all_gather(adjoint, "dp", axis=0, tiled=True))
    sums_out = accumulate(
        own_hidden, sq_hidden, lax.all_gather(output_adjoint, "dp", axis=0, tiled=True)
    )
    gradient_in, precond_in, term_in = finish(sums_in, total_rows)
    gradient_out, precond_out, term_out = finish(sums_out, total_rows)
    sq_norm = lax.psum(term_in + term_out, ("dp", "mp"))
    rescale = jnp.sqrt(2.0 * D * H / sq_norm)
    direction_in = gradient_in / precond_in * rescale
    direction_out = gradient_out / precond_out * rescale
    return (precond_in, direction_in, precond_out, direction_out, sq_norm)


def solution(mesh):
    placed = (P("dp", None), P("dp", "mp"), P("dp", "mp"), P("dp", "mp"))
    return jax.shard_map(
        shards,
        mesh=mesh,
        in_specs=placed,
        out_specs=(P("dp", "mp"), P("dp", "mp"), P("dp", "mp"), P("dp", "mp"), P()),
        check_vma=False,
    )
```

profile of v0, /device:TPU:0, one launch (start us, length us, event | category | flops | bytes accessed | tf_op | source)
XLA Modules:
  0.0 133.4 jit_solution(15350232104087235126)
XLA Ops:
  0.6 5.2 %all-to-all-start = ((bf16[4,8,1024]{2,0,1:T(4,128)(2,1)}), bf16[4,8,1024]{2,0,1:T(4,128)(2,1)S(1)}, u32[]{:S(2)}, u32[]{:S(2)}) async-start(bf16[4,8,1024]{2,0,1:T(4,128)(2,1)} %bitcast.22), calls=%async_computation | async-start | bytes 131072 | tf_op jit(solution)/shard_map/all_to_all | solution.py:42
  5.8 0.8 fusion.13
  6.6 14.1 %all_gather.10 = bf16[4,8192]{1,0:T(4,128)(2,1)} all-gather(bf16[4,2048]{1,0:T(4,128)(2,1)S(1)} %get-tuple-element.9), channel_id=1, replica_groups=mesh['dp'=8,'mp'=4] {'mp'}, dimensions={1}, use_global_device_ids=true | all-gather | bytes 81920 | tf_op jit(solution)/shard_map/all_gather | solution.py:45
  20.7 0.0 all-to-all-done
  20.7 4.3 %all-to-all-start.1 = ((bf16[4,8,1024]{2,0,1:T(4,128)(2,1)}), bf16[4,8,1024]{2,0,1:T(4,128)(2,1)S(1)}, u32[]{:S(2)}, u32[]{:S(2)}) async-start(bf16[4,8,1024]{2,0,1:T(4,128)(2,1)} %bitcast.4), calls=%async_computation.1 | async-start | bytes 131072 | tf_op jit(solution)/shard_map/all_to_all | solution.py:46
  25.0 9.7 %all-gather = bf16[8,4,2048]{2,1,0:T(4,128)(2,1)S(1)} all-gather(bf16[1,4,2048]{2,1,0:T(4,128)(2,1)S(1)} %get-tuple-element.10), channel_id=1, replica_groups=mesh['dp'=8,'mp'=4] {'dp'}, dimensions={0}, use_global_device_ids=true | all-gather | bytes 147456 | tf_op jit(solution)/shard_map/all_gather | solution.py:48
  34.7 9.2 %all-gather.1 = bf16[8,4,2048]{2,1,0:T(4,128)(2,1)S(1)} all-gather(bf16[1,4,2048]{2,1,0:T(4,128)(2,1)} %bitcast.23), channel_id=1, replica_groups=mesh['dp'=8,'mp'=4] {'dp'}, dimensions={0}, use_global_device_ids=true | all-gather | bytes 147456 | tf_op jit(solution)/shard_map/all_gather | solution.py:50
  44.0 0.0 all-to-all-done.1
  44.0 1.3 fusion.6
  45.3 0.0 copy-start
  45.3 7.8 %multiply_reduce_fusion = (f32[]{:T(128)}, f32[1024,2048]{1,0:T(8,128)}) fusion(f32[1024,2048]{1,0:T(8,128)S(1)} %fusion.6, bf16[32,1024]{1,0:T(8,128)(2,1)S(1)} %all_to_all.35, bf16[32,2048]{1,0:T(8,128)(2,1)S(1)} %reshape.19), kind=kOutput, calls=%fused_computation.6 | convolution fusion | flops 146800640 | bytes 16973828 | tf_op jit(solution)/shard_map/dot_general | solution.py:21
  53.1 0.0 copy-done
  53.1 1.3 fusion.5
  54.3 0.0 copy-start.1
  54.4 7.7 %fusion.2 = (f32[]{:T(128)}, f32[2048,1024]{0,1:T(8,128)}) fusion(f32[1024,2048]{1,0:T(8,128)S(1)} %fusion.5, bf16[32,2048]{1,0:T(8,128)(2,1)S(1)} %reshape.17, bf16[32,1024]{1,0:T(8,128)(2,1)S(1)} %all_to_all.31), kind=kOutput, calls=%fused_computation.4 | convolution fusion | flops 146800640 | bytes 16973828 | tf_op jit(solution)/shard_map/dot_general | solution.py:21
  62.0 0.0 copy-done.1
  63.3 39.4 %psum.7 = f32[]{:T(128)} all-reduce(f32[]{:T(128)S(6)} %add.21), channel_id=1, replica_groups=mesh['dp'=8,'mp'=4] {'dp','mp'}, use_global_device_ids=true, to_apply=%region_2.0 | all-reduce | flops 1 | bytes 8 | tf_op jit(solution)/shard_map/psum | solution.py:54
  103.5 29.9 %fusion = (f32[1024,2048]{1,0:T(8,128)}, f32[1024,2048]{1,0:T(8,128)}, f32[1024,2048]{1,0:T(8,128)}, f32[1024,2048]{1,0:T(8,128)}) fusion(f32[2048,1024]{0,1:T(8,128)} %get-tuple-element.12, f32[1024,2048]{1,0:T(8,128)} %copy-done.1, f32[]{:T(128)S(6)} %sqrt.3, f32[1024,2048]{1,0:T(8,128)} %copy-done, f32[1024,2048]{1,0:T(8,128)} %get-tuple-element.14), kind=kLoop, calls=%fused_computation.2 | loop fusion | flops 20971520 | bytes 67108864 | tf_op jit(solution)/shard_map/mul | solution.py:56
  (4 shorter events, 0.1 us)
Async XLA Ops:
  0.6 20.1 %all-to-all-start = ((bf16[4,8,1024]{2,0,1:T(4,128)(2,1)}), bf16[4,8,1024]{2,0,1:T(4,128)(2,1)S(1)}, u32[]{:S(2)}, u32[]{:S(2)}) async-start(bf16[4,8,1024]{2,0,1:T(4,128)(2,1)} %bitcast.22), calls=%async_computation | async-start | bytes 131072 | tf_op jit(solution)/shard_map/all_to_all | solution.py:42
  20.7 23.2 %all-to-all-start.1 = ((bf16[4,8,1024]{2,0,1:T(4,128)(2,1)}), bf16[4,8,1024]{2,0,1:T(4,128)(2,1)S(1)}, u32[]{:S(2)}, u32[]{:S(2)}) async-start(bf16[4,8,1024]{2,0,1:T(4,128)(2,1)} %bitcast.4), calls=%async_computation.1 | async-start | bytes 131072 | tf_op jit(solution)/shard_map/all_to_all | solution.py:46
  45.3 7.8 %copy-start = (f32[1024,2048]{1,0:T(8,128)}, f32[1024,2048]{1,0:T(8,128)S(1)}, u32[]{:S(2)}) copy-start(f32[1024,2048]{1,0:T(8,128)S(1)} %fusion.6) | copy-start | bytes 25165828
  54.3 7.7 %copy-start.1 = (f32[1024,2048]{1,0:T(8,128)}, f32[1024,2048]{1,0:T(8,128)S(1)}, u32[]{:S(2)}) copy-start(f32[1024,2048]{1,0:T(8,128)S(1)} %fusion.5) | copy-start | bytes 25165828
where the time goes:
time: 134 us; the launch traced here: 133 us
  blocking collectives  72.4 us (54%)
  other arithmetic  30.6 us (23%)
  matrix products  18 us (13%)
  starting transfers between devices  9.48 us (7%)
  between operations  2.7 us (2%)
    psum x1, blocking collectives, shards(): sq_norm = lax.psum(term_in + term_out, ('dp', 'mp'))  39.4 us
    mul x1, other arithmetic, shards(): direction_in = gradient_in / precond_in * rescale  29.9 us
    dot_general x2, matrix products, accumulate(): lax.dot_general(act_block, adj_piece, contract, preferred_element_type=jn...  15.4 us
    all_gather x1, blocking collectives, shards(): wide_hidden = lax.all_gather(hidden, 'mp', axis=1, tiled=True)  14.1 us
    all_gather x1, blocking collectives, shards(): lax.all_gather(adjoint, 'dp', axis=0, tiled=True)  9.71 us
    all_gather x1, blocking collectives, shards(): lax.all_gather(output_adjoint, 'dp', axis=0, tiled=True)  9.16 us
    all_to_all x1, starting transfers between devices, shards(): lax.all_to_all(layer_input, 'dp', split_axis=1, concat_axis=0, tiled=True)  5.21 us
    all_to_all x1, starting transfers between devices, shards(): lax.all_to_all(wide_hidden, 'dp', split_axis=1, concat_axis=0, tiled=True)  4.27 us
  transfers between devices with their start and end apart: 2, of which 0 were waited for; matrix products, arithmetic and copies ran while one was open for 1% of the time, Pallas kernels for 0%

commit v1 on v0

v1 whole, which is shorter than its diff:
```python
import functools

import jax
import jax.numpy as jnp
from jax import lax
from jax.experimental import pallas as pl
from jax.experimental.pallas import tpu as pltpu
from jax.sharding import PartitionSpec as P

MESH = pl.DeviceIdType.MESH
VMEM = pl.BlockSpec(memory_space=pltpu.VMEM)

DAMPING = 0.1
WIDTH = 256


def aligned(index, size):
    return pl.ds(pl.multiple_of(index * size, size), size)


def gather_kernel(
    n, m, x_ref, pre_ref, hadj_ref, oadj_ref, x_out, h_out, a_out, o_out,
    hid, adj, x_in, h_in, a_in, o_in, wide, x_send, h_send, a_send, o_send, x_recv, h_recv, a_recv, o_recv,
):
    my_d, my_m = lax.axis_index("dp"), lax.axis_index("mp")
    share = n // m
    rows, own = x_ref.shape[0], x_out.shape[1]
    source_m = my_d // share

    barrier = pltpu.get_barrier_semaphore()
    for step in range(1, n):
        pl.semaphore_signal(
            barrier, inc=1, device_id=(lax.rem(my_d + step, n), my_m), device_id_type=MESH
        )

    @pl.when(source_m != my_m)
    def _():
        for d in range(n):
            pl.semaphore_signal(barrier, inc=1, device_id=(d, source_m), device_id_type=MESH)

    preact = pre_ref[...].astype(jnp.float32)
    logistic = jax.nn.sigmoid(preact)
    hid[...] = (preact * logistic).astype(jnp.bfloat16)
    adj[...] = (
        hadj_ref[...].astype(jnp.float32) * logistic * (1.0 + preact * (1.0 - logistic))
    ).astype(jnp.bfloat16)

    pl.semaphore_wait(barrier, (n - 1) + share * (m - 1))

    def remote(src, dst, send, recv, d, mm):
        return pltpu.make_async_remote_copy(
            src_ref=src, dst_ref=dst.at[my_d], send_sem=send, recv_sem=recv.at[my_d],
            device_id=(d, mm), device_id_type=MESH,
        )

    copies = []
    for step in range(1, n):
        d = lax.rem(my_d + step, n)
        copies.append(remote(x_ref.at[:, aligned(d, own)], x_in, x_send.at[step], x_recv, d, my_m))
        copies.append(remote(adj, a_in, a_send.at[step], a_recv, d, my_m))
    hidden_copies = []
    for j in range(share):
        for k in range(m):
            d = my_m * share + j
            copy = remote(
                hid.at[:, pl.ds(j * own, own)], h_in, h_send.at[j * m + k], h_recv, d, lax.rem(my_m + k, m)
            )
            hidden_copies.append((copy, (d != my_d) if k == 0 else None))
    late = []
    for step in range(1, n):
        d = lax.rem(my_d + step, n)
        late.append(remote(oadj_ref, o_in, o_send.at[step], o_recv, d, my_m))

    def each_hidden(act):
        for copy, condition in hidden_copies:
            if condition is None:
                act(copy)
            else:
                pl.when(condition)(functools.partial(act, copy))

    each_hidden(lambda copy: copy.start())
    for copy in copies + late:
        copy.start()

    x_in[my_d] = x_ref[:, aligned(my_d, own)]
    a_in[my_d] = adj[...]
    o_in[my_d] = oadj_ref[...]

    @pl.when(source_m == my_m)
    def _():
        h_in[my_d] = hid[:, aligned(lax.rem(my_d, share), own)]

    def arrived(buffer, recv, d):
        pltpu.make_async_copy(buffer.at[d], buffer.at[d], recv.at[d]).wait()

    for step in range(1, n):
        d = lax.rem(my_d + step, n)
        arrived(x_in, x_recv, d)
        arrived(a_in, a_recv, d)
        arrived(o_in, o_recv, d)
        arrived(h_in, h_recv, d)

    @pl.when(source_m != my_m)
    def _():
        arrived(h_in, h_recv, my_d)

    for landed, out in ((x_in, x_out), (h_in, h_out), (a_in, a_out), (o_in, o_out)):
        columns = out.shape[1]
        for d in range(n):
            wide[pl.ds(d * rows, rows), pl.ds(0, columns)] = landed[d].astype(jnp.float32)
        out[...] = wide[:, pl.ds(0, columns)].astype(jnp.bfloat16)

    for copy in copies + late:
        copy.wait_send()
    each_hidden(lambda copy: copy.wait_send())


def gather_plain(layer_input, pre_act, hidden_adjoint, output_adjoint):
    preact = pre_act.astype(jnp.float32)
    logistic = jax.nn.sigmoid(preact)
    hidden = (preact * logistic).astype(jnp.bfloat16)
    adjoint = (
        hidden_adjoint.astype(jnp.float32) * logistic * (1.0 + preact * (1.0 - logistic))
    ).astype(jnp.bfloat16)
    wide_hidden = lax.all_gather(hidden, "mp", axis=1, tiled=True)
    return (
        lax.all_to_all(layer_input, "dp", split_axis=1, concat_axis=0, tiled=True),
        lax.all_to_all(wide_hidden, "dp", split_axis=1, concat_axis=0, tiled=True),
        lax.all_gather(adjoint, "dp", axis=0, tiled=True),
        lax.all_gather(output_adjoint, "dp", axis=0, tiled=True),
    )


def square_bf(values):
    wide = values.astype(jnp.float32)
    return (wide * wide).astype(jnp.bfloat16)


def products(left, left_sq, right, total_rows):
    gradient = jnp.dot(left, right, preferred_element_type=jnp.float32) / total_rows
    squares = jnp.dot(left_sq, square_bf(right), preferred_element_type=jnp.float32) / total_rows
    damped = squares + DAMPING
    root = lax.rsqrt(damped)
    return gradient, damped, root, root * lax.rsqrt(root)


def turn(refs, turned, squared):
    @pl.when(pl.program_id(0) == 0)
    def _():
        for layer, ref in enumerate(refs):
            value = ref[...].astype(jnp.float32).T
            turned[layer] = value.astype(jnp.bfloat16)
            squared[layer] = (value * value).astype(jnp.bfloat16)


def precond_kernel(
    chunk, x_ref, h_ref, a_ref, o_ref, p_in, p_out, norm, turned, squared
):
    turn((x_ref, h_ref), turned, squared)
    total_rows = x_ref.shape[0]

    @pl.when(pl.program_id(0) == 0)
    def _():
        norm[...] = jnp.zeros_like(norm)

    for layer, (right_ref, out) in enumerate(((a_ref, p_in), (o_ref, p_out))):
        right = right_ref[...]
        total = norm[...]
        for start in range(0, out.shape[0], chunk):
            part = pl.ds(start, chunk)
            gradient, damped, root, mixed = products(
                turned[layer, part], squared[layer, part], right, total_rows
            )
            out[part, :] = damped * mixed
            term = gradient * gradient * (root * mixed)
            total = total + jnp.sum(term.reshape(chunk // 8, 8, term.shape[1]), axis=0)
        norm[...] = total


def reduce_kernel(n, m, part_ref, total_out, mine, slots, send, recv):
    my_d, my_m = lax.axis_index("dp"), lax.axis_index("mp")
    me = my_d * m + my_m
    count = n * m

    def other(step):
        peer = lax.rem(me + step, count)
        return peer, (peer // m, lax.rem(peer, m))

    barrier = pltpu.get_barrier_semaphore()
    for step in range(1, count):
        pl.semaphore_signal(barrier, inc=1, device_id=other(step)[1], device_id_type=MESH)
    column = jnp.sum(part_ref[...], axis=0, keepdims=True)
    narrow = column[:, :128]
    for start in range(128, column.shape[1], 128):
        narrow = narrow + column[:, start : start + 128]
    mine[...] = narrow
    slots[me] = narrow
    pl.semaphore_wait(barrier, count - 1)
    copies = []
    for step in range(1, count):
        copy = pltpu.make_async_remote_copy(
            src_ref=mine, dst_ref=slots.at[me], send_sem=send.at[step], recv_sem=recv.at[me],
            device_id=other(step)[1], device_id_type=MESH,
        )
        copy.start()
        copies.append(copy)
    for step in range(1, count):
        peer = other(step)[0]
        pltpu.make_async_copy(slots.at[peer], slots.at[peer], recv.at[peer]).wait()
    total = jnp.sum(slots[...], axis=0)
    total_out[...] = jnp.broadcast_to(jnp.sum(total, axis=1, keepdims=True), total_out.shape)
    for copy in copies:
        copy.wait_send()


def direction_kernel(
    chunk, entries, x_ref, h_ref, a_ref, o_ref, total_ref, d_in, d_out, norm_out, turned, squared
):
    turn((x_ref, h_ref), turned, squared)
    total_rows = x_ref.shape[0]
    norm_out[...] = total_ref[:, 0:1]
    rescale = jnp.sqrt(2.0 * entries / total_ref[:, 0:1])
    for layer, (right_ref, out) in enumerate(((a_ref, d_in), (o_ref, d_out))):
        right = right_ref[...]
        for start in range(0, out.shape[0], chunk):
            part = pl.ds(start, chunk)
            gradient, _, root, mixed = products(
                turned[layer, part], squared[layer, part], right, total_rows
            )
            out[part, :] = gradient * (root * mixed) * rescale


def shards(n, m, layer_input, pre_act, hidden_adjoint, output_adjoint):
    rows, width = layer_input.shape
    local = pre_act.shape[1]
    own = width // n
    examples = rows * n
    chunk = min(own, 128)
    bf = lambda *shape: jax.ShapeDtypeStruct(shape, jnp.bfloat16)
    sems = pltpu.SemaphoreType.DMA

    direct = own % 128 == 0
    if direct:
        gathered = pl.pallas_call(
            functools.partial(gather_kernel, n, m),
            out_shape=(bf(examples, own), bf(examples, own), bf(examples, local), bf(examples, local)),
            in_specs=[VMEM] * 4,
            out_specs=(VMEM,) * 4,
            scratch_shapes=[
                pltpu.VMEM((rows, local), jnp.bfloat16),
                pltpu.VMEM((rows, local), jnp.bfloat16),
                pltpu.VMEM((n, rows, own), jnp.bfloat16),
                pltpu.VMEM((n, rows, own), jnp.bfloat16),
                pltpu.VMEM((n, rows, local), jnp.bfloat16),
                pltpu.VMEM((n, rows, local), jnp.bfloat16),
                pltpu.VMEM((examples, local), jnp.float32),
            ]
            + [sems((n,)), sems((n,)), sems((n,)), sems((n,))]
            + [sems((n,))] * 4,
            compiler_params=pltpu.CompilerParams(
                collective_id=0, has_side_effects=True, vmem_limit_bytes=8 << 20
            ),
        )(layer_input, pre_act, hidden_adjoint, output_adjoint)
    else:
        gathered = gather_plain(layer_input, pre_act, hidden_adjoint, output_adjoint)

    whole = pl.BlockSpec((examples, own), lambda i: (0, 0))
    piece = pl.BlockSpec((examples, WIDTH), lambda i: (0, i))
    block = pl.BlockSpec((own, WIDTH), lambda i: (0, i))
    result = jax.ShapeDtypeStruct((own, local), jnp.float32)
    turned = [pltpu.VMEM((2, own, examples), jnp.bfloat16)] * 2
    local_params = pltpu.CompilerParams(
        dimension_semantics=("arbitrary",), vmem_limit_bytes=24 << 20
    )
    precond_in, precond_out, norm = pl.pallas_call(
        functools.partial(precond_kernel, chunk),
        grid=(local // WIDTH,),
        out_shape=(result, result, jax.ShapeDtypeStruct((8, WIDTH), jnp.float32)),
        in_specs=[whole, whole, piece, piece],
        out_specs=(block, block, pl.BlockSpec((8, WIDTH), lambda i: (0, 0))),
        scratch_shapes=turned,
        compiler_params=local_params,
    )(*gathered)

    if direct:
        total = pl.pallas_call(
            functools.partial(reduce_kernel, n, m),
            out_shape=jax.ShapeDtypeStruct((1, 128), jnp.float32),
            in_specs=[VMEM],
            out_specs=VMEM,
            scratch_shapes=[
                pltpu.VMEM((1, 128), jnp.float32),
                pltpu.VMEM((n * m, 1, 128), jnp.float32),
                sems((n * m,)),
                sems((n * m,)),
            ],
            compiler_params=pltpu.CompilerParams(
                collective_id=1, has_side_effects=True, vmem_limit_bytes=4 << 20
            ),
        )(norm)
    else:
        total = jnp.broadcast_to(lax.psum(jnp.sum(norm), ("dp", "mp")), (1, 128))

    direction_in, direction_out, sq_norm = pl.pallas_call(
        functools.partial(direction_kernel, chunk, float(width) * float(local * m)),
        grid=(local // WIDTH,),
        out_shape=(result, result, jax.ShapeDtypeStruct((1, 1), jnp.float32)),
        in_specs=[whole, whole, piece, piece, pl.BlockSpec((1, 128), lambda i: (0, 0))],
        out_specs=(block, block, pl.BlockSpec((1, 1), lambda i: (0, 0))),
        scratch_shapes=turned,
        compiler_params=local_params,
    )(*gathered, total)
    return (precond_in, direction_in, precond_out, direction_out, sq_norm.reshape(()))


def solution(mesh):
    placed = (P("dp", None), P("dp", "mp"), P("dp", "mp"), P("dp", "mp"))
    return jax.shard_map(
        functools.partial(shards, mesh.shape["dp"], mesh.shape["mp"]),
        mesh=mesh,
        in_specs=placed,
        out_specs=(P("dp", "mp"), P("dp", "mp"), P("dp", "mp"), P("dp", "mp"), P()),
        check_vma=False,
    )
```

time: 134 us -> 42.1 us (0.31)
  blocking collectives: 72.4 us -> 0 us
  Pallas kernels: 0 us -> 38 us
  other arithmetic: 30.6 us -> 0 us
  matrix products: 18 us -> 0 us
  starting transfers between devices: 9.48 us -> 0 us
  local copies, waits for them, and re-layouts: 0.12 us -> 2.98 us
  between operations: 2.7 us -> 0.66 us
    psum x1 -> x0, blocking collectives: 39.4 us -> none  [shards(): sq_norm = lax.psum(term_in + term_out, ('dp', 'mp'))]
    pallas_call x0 -> x4, Pallas kernels: none -> 38 us  [the longest x1 12.8 us: shards(): pl.pallas_call(functools.partial(gather_kernel, n, m), out_shape=(bf(exam...]
    all_gather x3 -> x0, blocking collectives: 33 us -> none  [the longest x1 14.1 us: shards(): wide_hidden = lax.all_gather(hidden, 'mp', axis=1, tiled=True)]
    mul x1 -> x0, other arithmetic: 29.9 us -> none  [shards(): direction_in = gradient_in / precond_in * rescale]
    dot_general x4 -> x0, matrix products: 18 us -> none  [the longest x2 15.4 us: accumulate(): lax.dot_general(act_block, adj_piece, contract, preferred_element_type=jn...]
    all_to_all x2 -> x0, starting transfers between devices: 9.48 us -> none  [the longest x1 5.21 us: shards(): lax.all_to_all(layer_input, 'dp', split_axis=1, concat_axis=0, tiled=True)]
    unnamed x6 -> x8, local copies, waits for them, and re-layouts: 0.08 us -> 2.98 us
  transfers between devices with their start and end apart: 2 -> 0, of which waited for: 0 -> 0; matrix products, arithmetic and copies ran while one was open for 1% -> 0% of each run, Pallas kernels for 0% -> 0%
where the time goes in v1:
time: 42.1 us; the launch traced here: 41.6 us
  Pallas kernels  38 us (90%)
  local copies, waits for them, and re-layouts  2.98 us (7%)
  between operations  0.66 us (2%)
    pallas_call x1, Pallas kernels, shards(): pl.pallas_call(functools.partial(gather_kernel, n, m), out_shape=(bf(exam...  12.8 us
    pallas_call x1, Pallas kernels, shards(): pl.pallas_call(functools.partial(precond_kernel, chunk), grid=(local // W...  8.75 us
    pallas_call x1, Pallas kernels, shards(): pl.pallas_call(functools.partial(direction_kernel, chunk, float(width) *...  8.23 us
    pallas_call x1, Pallas kernels, shards(): pl.pallas_call(functools.partial(reduce_kernel, n, m), out_shape=jax.Shap...  8.17 us
    unnamed x8, local copies, waits for them, and re-layouts  2.98 us

profile of v1, /device:TPU:0, one launch (start us, length us, event | category | flops | bytes accessed | tf_op | source)
XLA Modules:
  0.0 41.6 jit_solution(15334571958866100814)
XLA Ops:
  0.6 0.0 copy-start
  0.6 0.8 %copy-done = bf16[4,8192]{1,0:T(4,128)(2,1)S(1)} copy-done((bf16[4,8192]{1,0:T(4,128)(2,1)S(1)}, bf16[4,8192]{1,0:T(4,128)(2,1)}, u32[]{:S(2)}) %copy-start) | copy-done | bytes 65560
  1.5 0.0 copy-start.1
  1.5 0.7 %copy-done.1 = bf16[4,2048]{1,0:T(4,128)(2,1)S(1)} copy-done((bf16[4,2048]{1,0:T(4,128)(2,1)S(1)}, bf16[4,2048]{1,0:T(4,128)(2,1)}, u32[]{:S(2)}) %copy-start.1) | copy-done | bytes 16408
  2.2 0.0 copy-start.2
  2.2 0.7 %copy-done.2 = bf16[4,2048]{1,0:T(4,128)(2,1)S(1)} copy-done((bf16[4,2048]{1,0:T(4,128)(2,1)S(1)}, bf16[4,2048]{1,0:T(4,128)(2,1)}, u32[]{:S(2)}) %copy-start.2) | copy-done | bytes 16408
  2.9 0.0 copy-start.3
  2.9 0.7 %copy-done.3 = bf16[4,2048]{1,0:T(4,128)(2,1)S(1)} copy-done((bf16[4,2048]{1,0:T(4,128)(2,1)S(1)}, bf16[4,2048]{1,0:T(4,128)(2,1)}, u32[]{:S(2)}) %copy-start.3) | copy-done | bytes 16408
  3.6 12.8 %shard_map.83 = (bf16[32,1024]{1,0:T(8,128)(2,1)S(1)}, bf16[32,1024]{1,0:T(8,128)(2,1)S(1)}, bf16[32,2048]{1,0:T(8,128)(2,1)S(1)}, bf16[32,2048]{1,0:T(8,128)(2,1)S(1)}) custom-call(bf16[4,8192]{1,0:T(4,128)(2,1)S(1)} %copy-done, bf16[4,2048]{1,0:T(4,128)(2,1)S(1)} %copy-done.1, bf16[4,2048]{1,0:T(4,128)(2,1)S(1)} %copy-done.2, bf16[4,2048]{1,0:T(4,128)(2,1)S(1)} %copy-done.3), custom_call_target="tpu_custom_call" | custom-call | tf_op jit(solution)/shard_map/pallas_call | solution.py:244
  16.5 8.8 %shard_map.84 = (f32[1024,2048]{1,0:T(8,128)}, f32[1024,2048]{1,0:T(8,128)}, f32[8,256]{1,0:T(8,128)S(1)}) custom-call(bf16[32,1024]{1,0:T(8,128)(2,1)S(1)} %get-tuple-element.15.x_ref, bf16[32,1024]{1,0:T(8,128)(2,1)S(1)} %get-tuple-element.16.h_ref, bf16[32,2048]{1,0:T(8,128)(2,1)S(1)} %get-tuple-element.17.a_ref, bf16[32,2048]{1,0:T(8,128)(2,1)S(1)} %get-tuple-element.18.o_ref), custom_call_target="tpu_custom_call" | custom-call | tf_op jit(solution)/shard_map/pallas_call | solution.py:275
  25.2 8.2 %shard_map.85.total_ref = f32[1,128]{1,0:T(1,128)S(1)} custom-call(f32[8,256]{1,0:T(8,128)S(1)} %get-tuple-element.20.part_ref), custom_call_target="tpu_custom_call" | custom-call | tf_op jit(solution)/shard_map/pallas_call | solution.py:286
  33.4 8.2 %shard_map.86 = (f32[1024,2048]{1,0:T(8,128)}, f32[1024,2048]{1,0:T(8,128)}, f32[1,1]{1,0:T(1,128)}) custom-call(bf16[32,1024]{1,0:T(8,128)(2,1)S(1)} %get-tuple-element.15.x_ref, bf16[32,1024]{1,0:T(8,128)(2,1)S(1)} %get-tuple-element.16.h_ref, bf16[32,2048]{1,0:T(8,128)(2,1)S(1)} %get-tuple-element.17.a_ref, bf16[32,2048]{1,0:T(8,128)(2,1)S(1)} %get-tuple-element.18.o_ref, ...), custom_call_target="tpu_custom_call" | custom-call | tf_op jit(solution)/shard_map/pallas_call | solution.py:304
Async XLA Ops:
  0.6 0.8 %copy-start = (bf16[4,8192]{1,0:T(4,128)(2,1)S(1)}, bf16[4,8192]{1,0:T(4,128)(2,1)}, u32[]{:S(2)}) copy-start(bf16[4,8192]{1,0:T(4,128)(2,1)} %x_ref.1) | copy-start | bytes 196612
  1.5 0.7 %copy-start.1 = (bf16[4,2048]{1,0:T(4,128)(2,1)S(1)}, bf16[4,2048]{1,0:T(4,128)(2,1)}, u32[]{:S(2)}) copy-start(bf16[4,2048]{1,0:T(4,128)(2,1)} %pre_ref.1) | copy-start | bytes 49156
  2.2 0.7 %copy-start.2 = (bf16[4,2048]{1,0:T(4,128)(2,1)S(1)}, bf16[4,2048]{1,0:T(4,128)(2,1)}, u32[]{:S(2)}) copy-start(bf16[4,2048]{1,0:T(4,128)(2,1)} %hadj_ref.1) | copy-start | bytes 49156
  2.9 0.7 %copy-start.3 = (bf16[4,2048]{1,0:T(4,128)(2,1)S(1)}, bf16[4,2048]{1,0:T(4,128)(2,1)}, u32[]{:S(2)}) copy-start(bf16[4,2048]{1,0:T(4,128)(2,1)} %oadj_ref.1) | copy-start | bytes 49156

commit v2 on v0

v2 whole, which is shorter than its diff:
```python
import functools

import jax
import jax.numpy as jnp
from jax import lax
from jax.experimental import pallas as pl
from jax.experimental.pallas import tpu as pltpu
from jax.sharding import PartitionSpec as P

MESH = pl.DeviceIdType.MESH
VMEM = pl.BlockSpec(memory_space=pltpu.VMEM)

DAMPING = 0.1
WIDTH = 256


def aligned(index, size):
    return pl.ds(pl.multiple_of(index * size, size), size)


def square_bf(values):
    wide = values.astype(jnp.float32)
    return (wide * wide).astype(jnp.bfloat16)


def mean_operand(values, total_rows):
    if total_rows & (total_rows - 1):
        return values, 1.0 / total_rows
    return values * jnp.asarray(1.0 / total_rows, values.dtype), None


def mean_product(left, right, total_rows):
    operand, factor = mean_operand(right, total_rows)
    product = jnp.dot(left, operand, preferred_element_type=jnp.float32)
    return product if factor is None else product * factor


def block_terms(left, left_sq, right, right_sq, total_rows):
    gradient = mean_product(left, right, total_rows)
    damped = mean_product(left_sq, right_sq, total_rows) + DAMPING
    root = lax.rsqrt(damped)
    return gradient, damped, root, root * lax.rsqrt(root)


def turn(value, layer, turned, squared):
    across = value.T
    turned[layer] = across.astype(jnp.bfloat16)
    squared[layer] = (across * across).astype(jnp.bfloat16)


def norm_terms(layer, turned, squared, right_ref, chunk):
    total_rows, columns = right_ref.shape
    own = turned.shape[1]

    def step(i, total):
        right = right_ref[:, aligned(i, WIDTH)]
        right_sq = square_bf(right)
        for start in range(0, own, chunk):
            part = pl.ds(start, chunk)
            gradient, _, root, mixed = block_terms(
                turned[layer, part], squared[layer, part], right, right_sq, total_rows
            )
            term = gradient * gradient * (root * mixed)
            total = total + jnp.sum(term.reshape(chunk // 8, 8, WIDTH), axis=0)
        return total

    return lax.fori_loop(0, columns // WIDTH, step, jnp.zeros((8, WIDTH), jnp.float32))


def narrowed(total):
    column = jnp.sum(total, axis=0, keepdims=True)
    narrow = column[:, :128]
    for start in range(128, column.shape[1], 128):
        narrow = narrow + column[:, start : start + 128]
    return narrow


def gather_kernel(
    n, m, chunk, x_hbm, pre_hbm, hadj_hbm, oadj_hbm, x_out, h_out, a_out, o_out, total_out,
    x_ref, pre_ref, hadj_ref, oadj_ref, hid, adj, x_in, h_in, a_in, o_in, wide, turned, squared, mine, slots,
    loads, x_send, h_send, a_send, o_send, x_recv, h_recv, a_recv, o_recv, t_send, t_recv,
):
    my_d, my_m = lax.axis_index("dp"), lax.axis_index("mp")
    share, count = n // m, n * m
    me = my_d * m + my_m
    rows, own = x_ref.shape[0], x_out.shape[1]
    source_m = my_d // share

    local_loads = [
        pltpu.make_async_copy(source, target, loads.at[i])
        for i, (source, target) in enumerate(
            ((pre_hbm, pre_ref), (hadj_hbm, hadj_ref), (x_hbm, x_ref), (oadj_hbm, oadj_ref))
        )
    ]
    for load in local_loads:
        load.start()

    def other(step):
        peer = lax.rem(me + step, count)
        return peer, (peer // m, lax.rem(peer, m))

    barrier = pltpu.get_barrier_semaphore()
    for step in range(1, count):
        pl.semaphore_signal(barrier, inc=1, device_id=other(step)[1], device_id_type=MESH)

    for load in local_loads:
        load.wait()
    preact = pre_ref[...].astype(jnp.float32)
    logistic = jax.nn.sigmoid(preact)
    hid[...] = (preact * logistic).astype(jnp.bfloat16)
    adj[...] = (
        hadj_ref[...].astype(jnp.float32) * logistic * (1.0 + preact * (1.0 - logistic))
    ).astype(jnp.bfloat16)
    x_in[my_d] = x_ref[:, aligned(my_d, own)]
    a_in[my_d] = adj[...]
    o_in[my_d] = oadj_ref[...]

    @pl.when(source_m == my_m)
    def _():
        h_in[my_d] = hid[:, aligned(lax.rem(my_d, share), own)]

    pl.semaphore_wait(barrier, count - 1)

    def remote(src, dst, send, recv, d, mm):
        return pltpu.make_async_remote_copy(
            src_ref=src, dst_ref=dst.at[my_d], send_sem=send, recv_sem=recv.at[my_d],
            device_id=(d, mm), device_id_type=MESH,
        )

    early, late, hidden_copies = [], [], []
    for step in range(1, n):
        d = lax.rem(my_d + step, n)
        early.append(remote(x_ref.at[:, aligned(d, own)], x_in, x_send.at[step], x_recv, d, my_m))
        early.append(remote(adj, a_in, a_send.at[step], a_recv, d, my_m))
        late.append(remote(oadj_ref, o_in, o_send.at[step], o_recv, d, my_m))
    for j in range(share):
        for k in range(m):
            d = my_m * share + j
            copy = remote(
                hid.at[:, pl.ds(j * own, own)], h_in, h_send.at[j * m + k], h_recv, d, lax.rem(my_m + k, m)
            )
            hidden_copies.append((copy, (d != my_d) if k == 0 else None))

    def each_hidden(act):
        for copy, condition in hidden_copies:
            if condition is None:
                act(copy)
            else:
                pl.when(condition)(functools.partial(act, copy))

    for copy in early:
        copy.start()
    each_hidden(lambda copy: copy.start())
    for copy in late:
        copy.start()

    def arrived(buffer, recv, d):
        pltpu.make_async_copy(buffer.at[d], buffer.at[d], recv.at[d]).wait()

    def assemble(landed, out):
        columns = out.shape[1]
        for d in range(n):
            wide[pl.ds(d * rows, rows), pl.ds(0, columns)] = landed[d].astype(jnp.float32)
        value = wide[:, pl.ds(0, columns)]
        out[...] = value.astype(jnp.bfloat16)
        return value

    for step in range(1, n):
        d = lax.rem(my_d + step, n)
        arrived(x_in, x_recv, d)
        arrived(a_in, a_recv, d)
    turn(assemble(x_in, x_out), 0, turned, squared)
    assemble(a_in, a_out)
    total = norm_terms(0, turned, squared, a_out, chunk)

    for step in range(1, n):
        d = lax.rem(my_d + step, n)
        arrived(h_in, h_recv, d)
        arrived(o_in, o_recv, d)

    @pl.when(source_m != my_m)
    def _():
        arrived(h_in, h_recv, my_d)

    turn(assemble(h_in, h_out), 1, turned, squared)
    assemble(o_in, o_out)
    total = total + norm_terms(1, turned, squared, o_out, chunk)

    narrow = narrowed(total)
    mine[...] = narrow
    slots[me] = narrow
    sums = []
    for step in range(1, count):
        copy = pltpu.make_async_remote_copy(
            src_ref=mine, dst_ref=slots.at[me], send_sem=t_send.at[step], recv_sem=t_recv.at[me],
            device_id=other(step)[1], device_id_type=MESH,
        )
        copy.start()
        sums.append(copy)
    for copy in early + late:
        copy.wait_send()
    each_hidden(lambda copy: copy.wait_send())
    for step in range(1, count):
        arrived(slots, t_recv, other(step)[0])
    total = jnp.sum(slots[...], axis=0)
    total_out[...] = jnp.broadcast_to(jnp.sum(total, axis=1, keepdims=True), total_out.shape)
    for copy in sums:
        copy.wait_send()


def gather_plain(layer_input, pre_act, hidden_adjoint, output_adjoint):
    preact = pre_act.astype(jnp.float32)
    logistic = jax.nn.sigmoid(preact)
    hidden = (preact * logistic).astype(jnp.bfloat16)
    adjoint = (
        hidden_adjoint.astype(jnp.float32) * logistic * (1.0 + preact * (1.0 - logistic))
    ).astype(jnp.bfloat16)
    wide_hidden = lax.all_gather(hidden, "mp", axis=1, tiled=True)
    return (
        lax.all_to_all(layer_input, "dp", split_axis=1, concat_axis=0, tiled=True),
        lax.all_to_all(wide_hidden, "dp", split_axis=1, concat_axis=0, tiled=True),
        lax.all_gather(adjoint, "dp", axis=0, tiled=True),
        lax.all_gather(output_adjoint, "dp", axis=0, tiled=True),
    )


def norm_kernel(chunk, x_ref, h_ref, a_ref, o_ref, norm, turned, squared):
    for layer, (left_ref, right_ref) in enumerate(((x_ref, a_ref), (h_ref, o_ref))):
        turn(left_ref[...].astype(jnp.float32), layer, turned, squared)
        terms = norm_terms(layer, turned, squared, right_ref, chunk)
        norm[...] = terms if layer == 0 else norm[...] + terms


def write_kernel(
    chunk, entries, x_ref, h_ref, a_ref, o_ref, total_ref, p_in, d_in, p_out, d_out, norm_out, turned, squared
):
    column, row = pl.program_id(0), pl.program_id(1)

    @pl.when((column == 0) & (row == 0))
    def _():
        norm_out[...] = total_ref[:, 0:1]
        for layer, ref in enumerate((x_ref, h_ref)):
            turn(ref[...].astype(jnp.float32), layer, turned, squared)

    total_rows = x_ref.shape[0]
    rescale = jnp.sqrt(2.0 * entries / total_ref[:, 0:1])
    height = p_in.shape[0]
    for layer, (right_ref, precond, direction) in enumerate(((a_ref, p_in, d_in), (o_ref, p_out, d_out))):
        right = right_ref[:, aligned(column, WIDTH)]
        right_sq = square_bf(right)
        for start in range(0, height, chunk):
            part = pl.ds(start, chunk)
            source = pl.ds(pl.multiple_of(row * height + start, chunk), chunk)
            gradient, damped, root, mixed = block_terms(
                turned[layer, source], squared[layer, source], right, right_sq, total_rows
            )
            precond[part, :] = damped * mixed
            direction[part, :] = gradient * (root * mixed) * rescale


def shards(n, m, layer_input, pre_act, hidden_adjoint, output_adjoint):
    rows, width = layer_input.shape
    local = pre_act.shape[1]
    own = width // n
    examples = rows * n
    chunk = min(own, 128)
    height = min(own, 512)
    bf = lambda *shape: jax.ShapeDtypeStruct(shape, jnp.bfloat16)
    vm = lambda *shape: pltpu.VMEM(shape, jnp.bfloat16)
    sems = pltpu.SemaphoreType.DMA
    turned = [vm(2, own, examples)] * 2
    local_params = pltpu.CompilerParams(vmem_limit_bytes=24 << 20)

    if own % 128 == 0:
        *gathered, total = pl.pallas_call(
            functools.partial(gather_kernel, n, m, chunk),
            out_shape=(
                bf(examples, own), bf(examples, own), bf(examples, local), bf(examples, local),
                jax.ShapeDtypeStruct((1, 128), jnp.float32),
            ),
            in_specs=[pl.BlockSpec(memory_space=pltpu.HBM)] * 4,
            out_specs=(VMEM,) * 5,
            scratch_shapes=[
                vm(rows, width), vm(rows, local), vm(rows, local), vm(rows, local),
                vm(rows, local), vm(rows, local),
                vm(n, rows, own), vm(n, rows, own), vm(n, rows, local), vm(n, rows, local),
                pltpu.VMEM((examples, local), jnp.float32),
                *turned,
                pltpu.VMEM((1, 128), jnp.float32),
                pltpu.VMEM((n * m, 1, 128), jnp.float32),
                sems((4,)),
            ]
            + [sems((n,))] * 8
            + [sems((n * m,))] * 2,
            compiler_params=pltpu.CompilerParams(
                collective_id=0, has_side_effects=True, vmem_limit_bytes=16 << 20
            ),
        )(layer_input, pre_act, hidden_adjoint, output_adjoint)
    else:
        gathered = gather_plain(layer_input, pre_act, hidden_adjoint, output_adjoint)
        norm = pl.pallas_call(
            functools.partial(norm_kernel, chunk),
            out_shape=jax.ShapeDtypeStruct((8, WIDTH), jnp.float32),
            in_specs=[VMEM] * 4,
            out_specs=VMEM,
            scratch_shapes=turned,
            compiler_params=local_params,
        )(*gathered)
        total = jnp.broadcast_to(lax.psum(jnp.sum(norm), ("dp", "mp")), (1, 128))

    block = pl.BlockSpec((height, WIDTH), lambda i, j: (j, i))
    result = jax.ShapeDtypeStruct((own, local), jnp.float32)
    *results, sq_norm = pl.pallas_call(
        functools.partial(write_kernel, chunk, float(width) * float(local * m)),
        grid=(local // WIDTH, own // height),
        out_shape=(result,) * 4 + (jax.ShapeDtypeStruct((1, 1), jnp.float32),),
        in_specs=[VMEM] * 5,
        out_specs=(block,) * 4 + (pl.BlockSpec((1, 1), lambda i, j: (0, 0)),),
        scratch_shapes=turned,
        compiler_params=local_params,
    )(*gathered, total)
    return (*results, sq_norm.reshape(()))


def solution(mesh):
    placed = (P("dp", None), P("dp", "mp"), P("dp", "mp"), P("dp", "mp"))
    return jax.shard_map(
        functools.partial(shards, mesh.shape["dp"], mesh.shape["mp"]),
        mesh=mesh,
        in_specs=placed,
        out_specs=(P("dp", "mp"), P("dp", "mp"), P("dp", "mp"), P("dp", "mp"), P()),
        check_vma=False,
    )
```

time: 134 us -> 41.9 us (0.31)
  blocking collectives: 72.4 us -> 0 us
  Pallas kernels: 0 us -> 37.9 us
  other arithmetic: 30.6 us -> 0 us
  matrix products: 18 us -> 0 us
  starting transfers between devices: 9.48 us -> 0 us
  local copies, waits for them, and re-layouts: 0.12 us -> 2.98 us
  between operations: 2.7 us -> 0.65 us
    psum x1 -> x0, blocking collectives: 39.4 us -> none  [shards(): sq_norm = lax.psum(term_in + term_out, ('dp', 'mp'))]
    pallas_call x0 -> x2, Pallas kernels: none -> 37.9 us  [the longest x1 24.2 us: shards(): pl.pallas_call(functools.partial(gather_kernel, n, m, chunk), out_shape=(...]
    all_gather x3 -> x0, blocking collectives: 33 us -> none  [the longest x1 14.1 us: shards(): wide_hidden = lax.all_gather(hidden, 'mp', axis=1, tiled=True)]
    mul x1 -> x0, other arithmetic: 29.9 us -> none  [shards(): direction_in = gradient_in / precond_in * rescale]
    dot_general x4 -> x0, matrix products: 18 us -> none  [the longest x2 15.4 us: accumulate(): lax.dot_general(act_block, adj_piece, contract, preferred_element_type=jn...]
    all_to_all x2 -> x0, starting transfers between devices: 9.48 us -> none  [the longest x1 5.21 us: shards(): lax.all_to_all(layer_input, 'dp', split_axis=1, concat_axis=0, tiled=True)]
    unnamed x6 -> x8, local copies, waits for them, and re-layouts: 0.08 us -> 2.98 us
  transfers between devices with their start and end apart: 2 -> 0, of which waited for: 0 -> 0; matrix products, arithmetic and copies ran while one was open for 1% -> 0% of each run, Pallas kernels for 0% -> 0%
where the time goes in v2:
time: 41.9 us; the launch traced here: 41.5 us
  Pallas kernels  37.9 us (90%)
  local copies, waits for them, and re-layouts  2.98 us (7%)
  between operations  0.65 us (2%)
    pallas_call x1, Pallas kernels, shards(): pl.pallas_call(functools.partial(gather_kernel, n, m, chunk), out_shape=(...  24.2 us
    pallas_call x1, Pallas kernels, shards(): pl.pallas_call(functools.partial(write_kernel, chunk, float(width) * floa...  13.7 us
    unnamed x8, local copies, waits for them, and re-layouts  2.98 us

profile of v2, /device:TPU:0, one launch (start us, length us, event | category | flops | bytes accessed | tf_op | source)
XLA Modules:
  0.0 41.5 jit_solution(9689409445512231985)
XLA Ops:
  0.6 0.0 copy-start
  0.6 0.8 %copy-done = bf16[4,8192]{1,0:T(4,128)(2,1)S(1)} copy-done((bf16[4,8192]{1,0:T(4,128)(2,1)S(1)}, bf16[4,8192]{1,0:T(4,128)(2,1)}, u32[]{:S(2)}) %copy-start) | copy-done | bytes 65560
  1.5 0.0 copy-start.1
  1.5 0.7 %copy-done.1 = bf16[4,2048]{1,0:T(4,128)(2,1)S(1)} copy-done((bf16[4,2048]{1,0:T(4,128)(2,1)S(1)}, bf16[4,2048]{1,0:T(4,128)(2,1)}, u32[]{:S(2)}) %copy-start.1) | copy-done | bytes 16408
  2.2 0.0 copy-start.2
  2.2 0.7 %copy-done.2 = bf16[4,2048]{1,0:T(4,128)(2,1)S(1)} copy-done((bf16[4,2048]{1,0:T(4,128)(2,1)S(1)}, bf16[4,2048]{1,0:T(4,128)(2,1)}, u32[]{:S(2)}) %copy-start.2) | copy-done | bytes 16408
  2.9 0.0 copy-start.3
  2.9 0.7 %copy-done.3 = bf16[4,2048]{1,0:T(4,128)(2,1)S(1)} copy-done((bf16[4,2048]{1,0:T(4,128)(2,1)S(1)}, bf16[4,2048]{1,0:T(4,128)(2,1)}, u32[]{:S(2)}) %copy-start.3) | copy-done | bytes 16408
  3.6 24.2 %shard_map.83 = (bf16[32,1024]{1,0:T(8,128)(2,1)S(1)}, bf16[32,1024]{1,0:T(8,128)(2,1)S(1)}, bf16[32,2048]{1,0:T(8,128)(2,1)S(1)}, bf16[32,2048]{1,0:T(8,128)(2,1)S(1)}, f32[1,128]{1,0:T(1,128)S(1)}) custom-call(bf16[4,8192]{1,0:T(4,128)(2,1)S(1)} %copy-done, bf16[4,2048]{1,0:T(4,128)(2,1)S(1)} %copy-done.1, bf16[4,2048]{1,0:T(4,128)(2,1)S(1)} %copy-done.2, ...), custom_call_target="tpu_custom_call" | custom-call | tf_op jit(solution)/shard_map/pallas_call | solution.py:275
  27.8 13.7 %shard_map.84 = (f32[1024,2048]{1,0:T(8,128)}, f32[1024,2048]{1,0:T(8,128)}, f32[1024,2048]{1,0:T(8,128)}, f32[1024,2048]{1,0:T(8,128)}, f32[1,1]{1,0:T(1,128)}) custom-call(bf16[32,1024]{1,0:T(8,128)(2,1)S(1)} %get-tuple-element.15.x_ref, bf16[32,1024]{1,0:T(8,128)(2,1)S(1)} %get-tuple-element.16.h_ref, bf16[32,2048]{1,0:T(8,128)(2,1)S(1)} %get-tuple-element.17.a_ref, ...), custom_call_target="tpu_custom_call" | custom-call | tf_op jit(solution)/shard_map/pallas_call | solution.py:313
Async XLA Ops:
  0.6 0.8 %copy-start = (bf16[4,8192]{1,0:T(4,128)(2,1)S(1)}, bf16[4,8192]{1,0:T(4,128)(2,1)}, u32[]{:S(2)}) copy-start(bf16[4,8192]{1,0:T(4,128)(2,1)} %x_hbm.1) | copy-start | bytes 196612
  1.5 0.7 %copy-start.1 = (bf16[4,2048]{1,0:T(4,128)(2,1)S(1)}, bf16[4,2048]{1,0:T(4,128)(2,1)}, u32[]{:S(2)}) copy-start(bf16[4,2048]{1,0:T(4,128)(2,1)} %pre_hbm.1) | copy-start | bytes 49156
  2.2 0.7 %copy-start.2 = (bf16[4,2048]{1,0:T(4,128)(2,1)S(1)}, bf16[4,2048]{1,0:T(4,128)(2,1)}, u32[]{:S(2)}) copy-start(bf16[4,2048]{1,0:T(4,128)(2,1)} %hadj_hbm.1) | copy-start | bytes 49156
  2.9 0.7 %copy-start.3 = (bf16[4,2048]{1,0:T(4,128)(2,1)S(1)}, bf16[4,2048]{1,0:T(4,128)(2,1)}, u32[]{:S(2)}) copy-start(bf16[4,2048]{1,0:T(4,128)(2,1)} %oadj_hbm.1) | copy-start | bytes 49156

commit v3 on v2

--- a/solution.py
+++ b/solution.py
@@ -76,9 +76,9 @@
 
 
 def gather_kernel(
-    n, m, chunk, x_hbm, pre_hbm, hadj_hbm, oadj_hbm, x_out, h_out, a_out, o_out, total_out,
-    x_ref, pre_ref, hadj_ref, oadj_ref, hid, adj, x_in, h_in, a_in, o_in, wide, turned, squared, mine, slots,
-    loads, x_send, h_send, a_send, o_send, x_recv, h_recv, a_recv, o_recv, t_send, t_recv,
+    n, m, chunk, x_hbm, pre_hbm, hadj_hbm, oadj_hbm, x_dst, h_dst, a_dst, o_dst, total_out,
+    x_out, h_out, a_out, o_out, x_ref, pre_ref, hadj_ref, oadj_ref, hid, adj, x_in, h_in, a_in, o_in, wide, turned, squared, mine, slots,
+    loads, stores, x_send, h_send, a_send, o_send, x_recv, h_recv, a_recv, o_recv, t_send, t_recv,
 ):
     my_d, my_m = lax.axis_index("dp"), lax.axis_index("mp")
     share, count = n // m, n * m
@@ -150,6 +150,8 @@
 
     for copy in early:
         copy.start()
+    for copy in early:
+        copy.wait_send()
     each_hidden(lambda copy: copy.start())
     for copy in late:
         copy.start()
@@ -165,12 +167,20 @@
         out[...] = value.astype(jnp.bfloat16)
         return value
 
+    stored = [
+        pltpu.make_async_copy(source, target, stores.at[i])
+        for i, (source, target) in enumerate(
+            ((x_out, x_dst), (a_out, a_dst), (h_out, h_dst), (o_out, o_dst))
+        )
+    ]
     for step in range(1, n):
         d = lax.rem(my_d + step, n)
         arrived(x_in, x_recv, d)
         arrived(a_in, a_recv, d)
     turn(assemble(x_in, x_out), 0, turned, squared)
     assemble(a_in, a_out)
+    stored[0].start()
+    stored[1].start()
     total = norm_terms(0, turned, squared, a_out, chunk)
 
     for step in range(1, n):
@@ -184,6 +194,8 @@
 
     turn(assemble(h_in, h_out), 1, turned, squared)
     assemble(o_in, o_out)
+    stored[2].start()
+    stored[3].start()
     total = total + norm_terms(1, turned, squared, o_out, chunk)
 
     narrow = narrowed(total)
@@ -197,9 +209,11 @@
         )
         copy.start()
         sums.append(copy)
-    for copy in early + late:
+    for copy in late:
         copy.wait_send()
     each_hidden(lambda copy: copy.wait_send())
+    for copy in stored:
+        copy.wait()
     for step in range(1, count):
         arrived(slots, t_recv, other(step)[0])
     total = jnp.sum(slots[...], axis=0)
@@ -232,12 +246,23 @@
 
 
 def write_kernel(
-    chunk, entries, x_ref, h_ref, a_ref, o_ref, total_ref, p_in, d_in, p_out, d_out, norm_out, turned, squared
+    chunk, entries, x_hbm, h_hbm, a_hbm, o_hbm, total_hbm, p_in, d_in, p_out, d_out, norm_out,
+    x_ref, h_ref, a_ref, o_ref, total_ref, turned, squared, loads,
 ):
     column, row = pl.program_id(0), pl.program_id(1)
 
     @pl.when((column == 0) & (row == 0))
     def _():
+        sources = (x_hbm, h_hbm, a_hbm, o_hbm, total_hbm)
+        targets = (x_ref, h_ref, a_ref, o_ref, total_ref)
+        copies = [
+            pltpu.make_async_copy(source, target, loads.at[i])
+            for i, (source, target) in enumerate(zip(sources, targets))
+        ]
+        for copy in copies:
+            copy.start()
+        for copy in copies:
+            copy.wait()
         norm_out[...] = total_ref[:, 0:1]
         for layer, ref in enumerate((x_ref, h_ref)):
             turn(ref[...].astype(jnp.float32), layer, turned, squared)
@@ -269,7 +294,7 @@
     vm = lambda *shape: pltpu.VMEM(shape, jnp.bfloat16)
     sems = pltpu.SemaphoreType.DMA
     turned = [vm(2, own, examples)] * 2
-    local_params = pltpu.CompilerParams(vmem_limit_bytes=24 << 20)
+    local_params = pltpu.CompilerParams(vmem_limit_bytes=63 << 20)
 
     if own % 128 == 0:
         *gathered, total = pl.pallas_call(
@@ -279,8 +304,9 @@
                 jax.ShapeDtypeStruct((1, 128), jnp.float32),
             ),
             in_specs=[pl.BlockSpec(memory_space=pltpu.HBM)] * 4,
-            out_specs=(VMEM,) * 5,
+            out_specs=(pl.BlockSpec(memory_space=pltpu.HBM),) * 4 + (VMEM,),
             scratch_shapes=[
+                vm(examples, own), vm(examples, own), vm(examples, local), vm(examples, local),
                 vm(rows, width), vm(rows, local), vm(rows, local), vm(rows, local),
                 vm(rows, local), vm(rows, local),
                 vm(n, rows, own), vm(n, rows, own), vm(n, rows, local), vm(n, rows, local),
@@ -289,11 +315,12 @@
                 pltpu.VMEM((1, 128), jnp.float32),
                 pltpu.VMEM((n * m, 1, 128), jnp.float32),
                 sems((4,)),
+                sems((4,)),
             ]
             + [sems((n,))] * 8
             + [sems((n * m,))] * 2,
             compiler_params=pltpu.CompilerParams(
-                collective_id=0, has_side_effects=True, vmem_limit_bytes=16 << 20
+                collective_id=0, has_side_effects=True, vmem_limit_bytes=63 << 20
             ),
         )(layer_input, pre_act, hidden_adjoint, output_adjoint)
     else:
@@ -314,9 +341,14 @@
         functools.partial(write_kernel, chunk, float(width) * float(local * m)),
         grid=(local // WIDTH, own // height),
         out_shape=(result,) * 4 + (jax.ShapeDtypeStruct((1, 1), jnp.float32),),
-        in_specs=[VMEM] * 5,
+        in_specs=[pl.BlockSpec(memory_space=pltpu.HBM)] * 5,
         out_specs=(block,) * 4 + (pl.BlockSpec((1, 1), lambda i, j: (0, 0)),),
-        scratch_shapes=turned,
+        scratch_shapes=[
+            vm(examples, own), vm(examples, own), vm(examples, local), vm(examples, local),
+            pltpu.VMEM((1, 128), jnp.float32),
+            *turned,
+            sems((5,)),
+        ],
         compiler_params=local_params,
     )(*gathered, total)
     return (*results, sq_norm.reshape(()))

time: 41.9 us -> 39.7 us (0.947)
  local copies, waits for them, and re-layouts: 2.98 us -> 0 us
  Pallas kernels: 37.9 us -> 38.8 us
    unnamed x8 -> x0, local copies, waits for them, and re-layouts: 2.98 us -> none
    pallas_call x1, Pallas kernels: 13.7 us -> 14.7 us  [shards(): pl.pallas_call(functools.partial(write_kernel, chunk, float(width) * floa...]
where the time goes in v3:
time: 39.7 us; the launch traced here: 39.5 us
  Pallas kernels  38.8 us (98%)
  between operations  0.64 us (2%)
    pallas_call x1, Pallas kernels, shards(): pl.pallas_call(functools.partial(gather_kernel, n, m, chunk), out_shape=(...  24.1 us
    pallas_call x1, Pallas kernels, shards(): pl.pallas_call(functools.partial(write_kernel, chunk, float(width) * floa...  14.7 us

profile of v3, /device:TPU:0, one launch (start us, length us, event | category | flops | bytes accessed | tf_op | source)
XLA Modules:
  0.0 39.5 jit_solution(6970876843942034868)
XLA Ops:
  0.6 24.1 %shard_map.83 = (bf16[32,1024]{1,0:T(8,128)(2,1)}, bf16[32,1024]{1,0:T(8,128)(2,1)}, bf16[32,2048]{1,0:T(8,128)(2,1)}, bf16[32,2048]{1,0:T(8,128)(2,1)}, f32[1,128]{1,0:T(1,128)}) custom-call(bf16[4,8192]{1,0:T(4,128)(2,1)} %x_hbm.1, bf16[4,2048]{1,0:T(4,128)(2,1)} %pre_hbm.1, bf16[4,2048]{1,0:T(4,128)(2,1)} %hadj_hbm.1, bf16[4,2048]{1,0:T(4,128)(2,1)} %oadj_hbm.1), custom_call_target="tpu_custom_call" | custom-call | tf_op jit(solution)/shard_map/pallas_call | solution.py:300
  24.8 14.7 %shard_map.84 = (f32[1024,2048]{1,0:T(8,128)}, f32[1024,2048]{1,0:T(8,128)}, f32[1024,2048]{1,0:T(8,128)}, f32[1024,2048]{1,0:T(8,128)}, f32[1,1]{1,0:T(1,128)}) custom-call(bf16[32,1024]{1,0:T(8,128)(2,1)} %get-tuple-element.15.x_hbm, bf16[32,1024]{1,0:T(8,128)(2,1)} %get-tuple-element.16.h_hbm, bf16[32,2048]{1,0:T(8,128)(2,1)} %get-tuple-element.17.a_hbm, ...), custom_call_target="tpu_custom_call" | custom-call | tf_op jit(solution)/shard_map/pallas_call | solution.py:340
